TPU v7x, 512 devices: a whole 4x8x8 slice. The times are simulated.
512 devices in a mesh: seq: 128 (over x, z_hi, y), tp: 4 (over z_lo, core).
Axes of the slice: x: 4, y: 8, z: 8 (z_hi: 4, z_lo: 2; z = z_hi * 2 + z_lo), core: 2. Of those that a mesh axis runs over, the one named last changes fastest.
Arguments:
- queries: bfloat16 [16384, 4096], P('seq', 'tp'), may hold values from -16 to 16
- keyvalues: bfloat16 [2, 16384, 1024], P(None, 'seq', 'tp'), may hold values from -16 to 16
- stretch_order: int32 [128], replicated, may hold values from 0 to 127, each once
- block_table: int32 [128, 128], replicated, may hold values 0 or 1
- proj_weight: bfloat16 [4096, 2048], P('tp'), may hold values from -0.09375 to 0.09375
Outputs:
- projected: bfloat16 [16384, 2048], P('seq', 'tp')
Inputs may be any that keep to these rules, and one draw needn't show every extreme that they name: `stretch_order`: every stretch number 0 to 127 appears once. `block_table`: entry [i, j] matters only where j < i.
All inputs are finite; a program needn't handle non-finite values.
Results may differ from a plain program's by a relative error of at most 0.014.
Values may be sent and summed in bfloat16 or wider, within the bound.
No kernel may reach another device: no remote copies, remote signals or barrier semaphores. Data moves between devices by JAX's collectives and lax.ppermute only.
A program may use at most 128 MiB of HBM per device.

v0:
```python
import functools

import jax
import jax.numpy as jnp
from jax import lax
from jax.experimental import pallas as pl
from jax.experimental.pallas import tpu as pltpu
from jax.sharding import PartitionSpec as P


HEAD = 128
ROWS = 128
NX, NZ, NY = 4, 4, 8
SCALE2 = 1.4426950408889634 / HEAD**0.5
NEG = -1e30
KEYS = 4


SMEM = pl.BlockSpec(memory_space=pltpu.SMEM)
VMEM = pl.BlockSpec(memory_space=pltpu.VMEM)
PARAMS = pltpu.CompilerParams(vmem_limit_bytes=26 * 1024 * 1024)


def _shift(a, dx=0, dz=0, dy=0):
    pairs = []
    for x in range(NX):
        for z in range(NZ):
            for y in range(NY):
                src = (x * NZ + z) * NY + y
                dst = (((x + dx) % NX) * NZ + (z + dz) % NZ) * NY + (y + dy) % NY
                pairs.append((src, dst))
    return lax.ppermute(a, "seq", pairs)


X_GROUPS = [[x * NZ * NY + r for x in range(NX)] for r in range(NZ * NY)]
Z_GROUPS = [[(x * NZ + z) * NY + y for z in range(NZ)] for x in range(NX) for y in range(NY)]


def _swap(a, groups):
    return lax.all_to_all(a, "seq", 0, 0, tiled=True, axis_index_groups=groups)


OTHERS = (1, 2, 3)
CALLS = {
    "att1": (OTHERS, (0, 7, 1)),
    "att2": (OTHERS, (6, 2)),
    "att3": (OTHERS, (5, 3)),
    "att4": (OTHERS, (4,)),
    "att_own": ((0,), (0, 7, 1, 6, 2, 5, 3, 4)),
}
PLACES = {}
LIST_END = 2
for _name, (_queries, _dists) in CALLS.items():
    for _j in range(len(_queries)):
        PLACES[_name, _j] = LIST_END
        LIST_END += 1 + len(_dists) * NZ + KEYS


def _lists_kernel(at_ref, order_ref, table_ref, out_ref):
    me = at_ref[0]
    x = lax.shift_right_logical(me, 5)
    z = lax.shift_right_logical(me, 3) & 3
    y = me & 7
    out_ref[0] = x
    out_ref[1] = z
    keys = {(d, n): order_ref[x * 32 + n * 8 + ((y + d) & 7)] for d in range(NY) for n in range(NZ)}
    for name, (queries, dists) in CALLS.items():
        for j, from_x in enumerate(queries):
            mine = order_ref[((x + from_x) & 3) * 32 + z * 8 + y]
            place = PLACES[name, j]
            count = jnp.int32(0)
            for c, d in enumerate(dists):
                for n in range(NZ):
                    key = keys[d, n]
                    out_ref[place + 1 + count] = c * NZ + n
                    count += jnp.where((key < mine) & (table_ref[mine, key] == 1), 1, 0)
            for n in range(KEYS - 1):
                out_ref[place + 1 + count + n] = 0
            out_ref[place] = count


def _lists(order, table):
    me = lax.axis_index("seq").astype(jnp.int32).reshape(1)
    return pl.pallas_call(
        _lists_kernel,
        in_specs=[SMEM, SMEM, SMEM],
        out_specs=SMEM,
        out_shape=jax.ShapeDtypeStruct((LIST_END,), jnp.int32),
        name="lists",
    )(me, order, table)


def _unit(q_ref, i, kv_ref, picks, bias, acc_ref, m_ref, j):
    def rows(part, g):
        return jnp.concatenate(
            [kv_ref[p, part * ROWS : (part + 1) * ROWS, g * HEAD : (g + 1) * HEAD] for p in picks], axis=0
        )

    scores = []
    for g in range(2):
        q = jnp.concatenate([q_ref[i, :, (g * 4 + h) * HEAD : (g * 4 + h + 1) * HEAD] for h in range(4)], axis=0)
        scores.append(
            lax.dot_general(q, rows(0, g), (((1,), (1,)), ((), ())), preferred_element_type=jnp.float32)
        )
    for g in range(2):
        v = rows(1, g)
        v = jnp.concatenate([v, jnp.ones_like(v)], axis=1)
        s = scores[g] * SCALE2 + bias
        heads = slice(g * 4, g * 4 + 4)
        m_old = m_ref[j, heads].reshape(4 * ROWS, HEAD)
        m_new = jnp.maximum(m_old, jnp.max(s, axis=1, keepdims=True))
        p = jnp.exp2(s - jnp.concatenate([m_new] * len(picks), axis=1))
        pv = jnp.dot(p.astype(jnp.bfloat16), v, preferred_element_type=jnp.float32)
        factor = jnp.exp2(m_old - m_new)
        acc = acc_ref[j, heads].reshape(4 * ROWS, 2 * HEAD)
        acc = acc * jnp.concatenate([factor, factor], axis=1) + pv
        acc_ref[j, heads] = acc.reshape(4, ROWS, 2 * HEAD)
        m_ref[j, heads] = m_new.reshape(4, ROWS, HEAD)


def _finish(acc_ref, m_ref, j, out_ref, i):
    col = lax.broadcasted_iota(jnp.int32, (ROWS, HEAD), 1) % 8
    sums = jnp.zeros((ROWS, HEAD), jnp.float32)
    tops = jnp.zeros((ROWS, HEAD), jnp.float32)
    for h in range(8):
        total = acc_ref[j, h, :, HEAD:]
        safe = jnp.where(total > 0.0, total, 1.0)
        out_ref[i, :, h * HEAD : (h + 1) * HEAD] = (acc_ref[j, h, :, :HEAD] / safe).astype(jnp.bfloat16)
        sums = jnp.where(col == h, total, sums)
        tops = jnp.where(col == h, m_ref[j, h], tops)
    some = sums > 0.0
    ext = jnp.where(some, tops + jnp.log2(jnp.where(some, sums, 1.0)), NEG)
    col = lax.broadcasted_iota(jnp.int32, (ROWS, HEAD), 1)
    hi = ext.astype(jnp.bfloat16).astype(jnp.float32)
    left = ext - hi
    mid = left.astype(jnp.bfloat16).astype(jnp.float32)
    ext = jnp.where(col < 8, hi, jnp.where(col < 16, mid, left - mid))
    out_ref[i, :, 8 * HEAD :] = ext.astype(jnp.bfloat16)


def _attend_kernel(*refs, name, first, last):
    queries, dists = CALLS[name]
    nq, nc = len(queries), len(dists)
    own = queries == (0,)
    list_ref, q_ref = refs[:2]
    chunk_refs = refs[2 : 2 + nc]
    rest = list(refs[2 + nc :])
    state = [] if first else [rest.pop(0), rest.pop(0)]
    kv_ref = rest.pop()
    if last:
        out_ref = rest.pop(0)
    acc_ref, m_ref = rest
    for c, ref in enumerate(chunk_refs):
        kv_ref[c * NZ : (c + 1) * NZ] = ref[...]
    if first:
        acc_ref[...] = jnp.zeros_like(acc_ref)
        m_ref[...] = jnp.full_like(m_ref, NEG)
    else:
        acc_ref[...] = state[0][...]
        m_ref[...] = state[1][...]
    if own:
        key = lax.broadcasted_iota(jnp.int32, (ROWS, ROWS), 1)
        row = lax.broadcasted_iota(jnp.int32, (ROWS, ROWS), 0)
        bias = jnp.concatenate([jnp.where(key > row, NEG, 0.0)] * 4, axis=0)
        _unit(q_ref, 0, kv_ref, [list_ref[1]], bias, acc_ref, m_ref, 0)
    lane = lax.broadcasted_iota(jnp.int32, (1, KEYS * ROWS), 1) // ROWS
    x = list_ref[0]
    step = PLACES[name, 1] - PLACES[name, 0] if nq > 1 else 0

    def where_q(j):
        return 0 if own else (x + queries[0] + j) & 3

    def each_query(j, carry):
        place = PLACES[name, 0] + j * step
        count = list_ref[place]

        def each(u, inner):
            picks = [list_ref[place + 1 + u * KEYS + n] for n in range(KEYS)]
            bias = jnp.where(lane + u * KEYS < count, 0.0, NEG)
            _unit(q_ref, where_q(j), kv_ref, picks, bias, acc_ref, m_ref, j)
            return inner

        lax.fori_loop(0, lax.shift_right_logical(count + KEYS - 1, KEYS.bit_length() - 1), each, 0)
        return carry

    if nq == 1:
        each_query(0, 0)
    else:
        lax.fori_loop(0, nq, each_query, 0)
    if last:
        for j in range(nq):
            _finish(acc_ref, m_ref, j, out_ref, where_q(j))


def _attend(name, lists, q, chunks, state, last):
    queries = CALLS[name][0]
    nq, nc = len(queries), len(chunks)
    first = state is None
    args = [lists, q, *chunks] + ([] if first else list(state))
    acc = jax.ShapeDtypeStruct((nq, 8, ROWS, 2 * HEAD), jnp.float32)
    top = jax.ShapeDtypeStruct((nq, 8, ROWS, HEAD), jnp.float32)
    scratch = [pltpu.VMEM((nc * NZ, 2 * ROWS, 2 * HEAD), jnp.bfloat16)]
    if last:
        out = (jax.ShapeDtypeStruct((q.shape[0], ROWS, 9 * HEAD), jnp.bfloat16),)
        scratch = [pltpu.VMEM(acc.shape, acc.dtype), pltpu.VMEM(top.shape, top.dtype)] + scratch
    else:
        out = (acc, top)
    pairs = nq * nc * NZ * 8
    got = pl.pallas_call(
        functools.partial(_attend_kernel, name=name, first=first, last=last),
        in_specs=[SMEM] + [VMEM] * (len(args) - 1),
        out_specs=tuple(VMEM for _ in out),
        out_shape=out,
        scratch_shapes=scratch,
        compiler_params=PARAMS,
        cost_estimate=pl.CostEstimate(
            flops=pairs * ROWS * ROWS * HEAD * 4, transcendentals=pairs * ROWS * ROWS, bytes_accessed=4 << 20
        ),
    )(*args)
    return got[0] if last else got


def _combine_kernel(at_ref, list_ref, own_ref, part_ref, w_ref, att_ref, out_ref):
    x = list_ref[0]
    lses = []
    for j in range(NX):
        ext = own_ref[0, :, 8 * HEAD :] if j == 0 else part_ref[(x + j) & 3, :, 8 * HEAD :]
        ext = ext.astype(jnp.float32)
        lses.append(ext[:, 0:8] + ext[:, 8:16] + ext[:, 16:24])
    top = functools.reduce(jnp.maximum, lses)
    ws = [jnp.exp2(v - top) for v in lses]
    total = functools.reduce(jnp.add, ws)
    ws = [w / total for w in ws]
    for h in range(8):
        at = slice(h * HEAD, (h + 1) * HEAD)
        mixed = ws[0][:, h : h + 1] * own_ref[0, :, at].astype(jnp.float32)
        for j in range(1, NX):
            mixed += ws[j][:, h : h + 1] * part_ref[(x + j) & 3, :, at].astype(jnp.float32)
        att_ref[:, at] = mixed.astype(jnp.bfloat16)
    _columns(at_ref, att_ref, w_ref, out_ref, 1)


def _columns(at_ref, att_ref, w_ref, out_ref, flip):
    me = at_ref[0]
    for n in range(2):
        at = pl.multiple_of((me ^ (2 * n + flip)) * 512, 512)
        out_ref[n] = jnp.dot(
            att_ref[...], w_ref[:, pl.ds(at, 512)], preferred_element_type=jnp.float32
        ).astype(out_ref.dtype)


def _keep_kernel(at_ref, att_ref, w_ref, out_ref):
    _columns(at_ref, att_ref, w_ref, out_ref, 0)


def _call(kernel, args, out, flops):
    many = isinstance(out, tuple)
    return pl.pallas_call(
        kernel,
        in_specs=[SMEM if a.dtype == jnp.int32 else VMEM for a in args],
        out_specs=tuple(VMEM for _ in out) if many else VMEM,
        out_shape=out,
        compiler_params=PARAMS,
        cost_estimate=pl.CostEstimate(flops=flops, transcendentals=0, bytes_accessed=5 << 20),
    )(*args)


def _ring(a, dy):
    return _shift(a, dy=dy)


def per_device(queries, keyvalues, stretch_order, block_table, proj_weight):
    kv = keyvalues.reshape(1, 2 * ROWS, 2 * HEAD)
    near = lax.all_gather(kv, "seq", axis=0, tiled=True, axis_index_groups=Z_GROUPS)
    q = _swap(jnp.broadcast_to(queries[None], (NX, ROWS, 8 * HEAD)), X_GROUPS)
    lists = _lists(stretch_order, block_table)
    f1, b1 = _ring(near, 1), _ring(near, -1)
    f2, b2 = _ring(f1, 1), _ring(b1, -1)
    state = _attend("att1", lists, q, [near, f1, b1], None, False)
    f3, b3 = _ring(f2, 1), _ring(b2, -1)
    state = _attend("att2", lists, q, [f2, b2], state, False)
    f4, b4 = _ring(f3[:2], 1), _ring(b3[2:], -1)
    state = _attend("att3", lists, q, [f3, b3], state, False)
    far = jnp.concatenate([f4, b4], axis=0)
    parts = _attend("att4", lists, q, [far], state, True)
    parts = _swap(parts, X_GROUPS)
    chunks = [near, f1, b1, f2, b2, f3, b3, far]
    own = _attend("att_own", lists, queries[None], chunks, None, True)
    me = lax.axis_index("tp").astype(jnp.int32).reshape(1)
    att, give = _call(
        _combine_kernel,
        [me, lists, own, parts, proj_weight],
        (jax.ShapeDtypeStruct((ROWS, 8 * HEAD), jnp.bfloat16), jax.ShapeDtypeStruct((2, ROWS, 512), jnp.bfloat16)),
        2 * ROWS * 1024 * 1024,
    )
    took = lax.ppermute(give, "tp", [(t, t ^ 1) for t in range(4)])
    keep = _call(
        _keep_kernel,
        [me, att, proj_weight],
        jax.ShapeDtypeStruct((2, ROWS, 512), jnp.float32),
        2 * ROWS * 1024 * 1024,
    )
    both = keep + took.astype(jnp.float32)
    beside = lax.ppermute(both[1].astype(jnp.bfloat16), "tp", [(t, t ^ 2) for t in range(4)])
    return (both[0] + beside.astype(jnp.float32)).astype(jnp.bfloat16)


def solution(mesh):
    in_specs = (P("seq", "tp"), P(None, "seq", "tp"), P(), P(), P("tp", None))
    return jax.shard_map(
        per_device, mesh=mesh, in_specs=in_specs, out_specs=P("seq", "tp"), check_vma=False
    )
```

profile of v0, /device:TPU:1, one launch (start us, length us, event | category | flops | bytes accessed | tf_op | source)
XLA Modules:
  0.0 136.8 jit_solution(5642662369441948819)
XLA Ops:
  0.0 21.5 %all_gather.3.refs_2_ = bf16[4,256,256]{2,1,0:T(8,128)(2,1)S(1)} all-gather(bf16[1,256,256]{2,1,0:T(8,128)(2,1)} %bitcast.13), channel_id=1, replica_groups={{0,32,64,96},{4,36,68,100},{8,40,72,104},{12,44,76,108},{16,48,80,112},..., dimensions={0}, use_global_device_ids=true | all-gather | bytes 655360 | tf_op jit(solution)/shard_map/all_gather | solution.py:274
  21.5 0.0 copy-start.4
  21.5 3.2 %collective-permute-start = (bf16[4,256,256]{2,1,0:T(8,128)(2,1)S(1)}, bf16[4,256,256]{2,1,0:T(8,128)(2,1)S(1)}, u32[]{:S(2)}, u32[]{:S(2)}) collective-permute-start(bf16[4,256,256]{2,1,0:T(8,128)(2,1)S(1)} %all_gather.3.refs_2_), channel_id=1, source_target_pairs={{0,4},{4,8},{8,12},{12,16},{16,20},{20,24},{24,28},{28,0},{32,36},... | collective-permute-start | bytes 1572872 | tf_op jit(solution)/shard_map/ppermute | solution.py:32
  24.7 3.8 %collective-permute-start.1 = (bf16[4,256,256]{2,1,0:T(8,128)(2,1)S(1)}, bf16[4,256,256]{2,1,0:T(8,128)(2,1)}, u32[]{:S(2)}, u32[]{:S(2)}) collective-permute-start(bf16[4,256,256]{2,1,0:T(8,128)(2,1)S(1)} %all_gather.3.refs_2_), channel_id=1, source_target_pairs={{0,28},{4,0},{8,4},{12,8},{16,12},{20,16},{24,20},{28,24},{32,60},... | collective-permute-start | bytes 1572872 | tf_op jit(solution)/shard_map/ppermute | solution.py:32
  28.5 8.5 %collective-permute-done.refs_3_ = bf16[4,256,256]{2,1,0:T(8,128)(2,1)S(1)} collective-permute-done((bf16[4,256,256]{2,1,0:T(8,128)(2,1)S(1)}, bf16[4,256,256]{2,1,0:T(8,128)(2,1)S(1)}, u32[]{:S(2)}, u32[]{:S(2)}) %collective-permute-start) | collective-permute-done | bytes 524320 | tf_op jit(solution)/shard_map/ppermute | solution.py:32
  37.0 0.0 copy-start.12
  37.0 1.9 %collective-permute-start.2 = (bf16[4,256,256]{2,1,0:T(8,128)(2,1)S(1)}, bf16[4,256,256]{2,1,0:T(8,128)(2,1)S(1)}, u32[]{:S(2)}, u32[]{:S(2)}) collective-permute-start(bf16[4,256,256]{2,1,0:T(8,128)(2,1)S(1)} %collective-permute-done.refs_3_), channel_id=1, source_target_pairs={{0,4},{4,8},{8,12},{12,16},{16,20},{20,24},{24,28},{28,0},{32,36},... | collective-permute-start | bytes 1572872 | tf_op jit(solution)/shard_map/ppermute | solution.py:32
  38.9 2.1 %broadcast_in_dim.10 = bf16[4,128,1024]{2,1,0:T(8,128)(2,1)} broadcast(bf16[128,1024]{1,0:T(8,128)(2,1)} %param.5), dimensions={1,2} | broadcast | bytes 1310720 | tf_op jit(solution)/shard_map/broadcast_in_dim | solution.py:275
  41.0 0.0 copy-done.4
  41.0 0.0 copy-done.12
  41.0 4.0 %all-to-all-start = ((bf16[4,128,1024]{2,1,0:T(8,128)(2,1)}), bf16[4,128,1024]{2,1,0:T(8,128)(2,1)S(1)}, u32[]{:S(2)}, u32[]{:S(2)}) async-start(bf16[4,128,1024]{2,1,0:T(8,128)(2,1)} %broadcast_in_dim.10), calls=%async_computation | async-start | bytes 2097152 | tf_op jit(solution)/shard_map/all_to_all | solution.py:40
  45.0 0.0 collective-permute-done.1.refs_4_
  45.0 4.6 %collective-permute-start.3 = (bf16[4,256,256]{2,1,0:T(8,128)(2,1)}, bf16[4,256,256]{2,1,0:T(8,128)(2,1)S(1)}, u32[]{:S(2)}, u32[]{:S(2)}) collective-permute-start(bf16[4,256,256]{2,1,0:T(8,128)(2,1)} %collective-permute-done.1.refs_4_), channel_id=1, source_target_pairs={{0,28},{4,0},{8,4},{12,8},{16,12},{20,16},{24,20},{28,24},{32,60},... | collective-permute-start | bytes 1572872 | tf_op jit(solution)/shard_map/ppermute | solution.py:32
  49.6 1.6 %collective-permute-done.2.refs_5_.refs_2_ = bf16[4,256,256]{2,1,0:T(8,128)(2,1)S(1)} collective-permute-done((bf16[4,256,256]{2,1,0:T(8,128)(2,1)S(1)}, bf16[4,256,256]{2,1,0:T(8,128)(2,1)S(1)}, u32[]{:S(2)}, u32[]{:S(2)}) %collective-permute-start.2) | collective-permute-done | bytes 524320 | tf_op jit(solution)/shard_map/ppermute | solution.py:32
  51.1 1.9 %collective-permute-start.4 = (bf16[4,256,256]{2,1,0:T(8,128)(2,1)S(1)}, bf16[4,256,256]{2,1,0:T(8,128)(2,1)S(1)}, u32[]{:S(2)}, u32[]{:S(2)}) collective-permute-start(bf16[4,256,256]{2,1,0:T(8,128)(2,1)S(1)} %collective-permute-done.2.refs_5_.refs_2_), channel_id=1, source_target_pairs={{0,4},{4,8},{8,12},{12,16},{16,20},{20,24},{24,28},{28,0},{32,36},... | collective-permute-start | bytes 1572872 | tf_op jit(solution)/shard_map/ppermute | solution.py:32
  53.1 5.1 %collective-permute-done.3.refs_6_.refs_3_ = bf16[4,256,256]{2,1,0:T(8,128)(2,1)S(1)} collective-permute-done((bf16[4,256,256]{2,1,0:T(8,128)(2,1)}, bf16[4,256,256]{2,1,0:T(8,128)(2,1)S(1)}, u32[]{:S(2)}, u32[]{:S(2)}) %collective-permute-start.3) | collective-permute-done | bytes 524320 | tf_op jit(solution)/shard_map/ppermute | solution.py:32
  58.2 0.0 copy-start.2
  58.2 5.2 %collective-permute-start.5 = (bf16[4,256,256]{2,1,0:T(8,128)(2,1)S(1)}, bf16[4,256,256]{2,1,0:T(8,128)(2,1)S(1)}, u32[]{:S(2)}, u32[]{:S(2)}) collective-permute-start(bf16[4,256,256]{2,1,0:T(8,128)(2,1)S(1)} %collective-permute-done.3.refs_6_.refs_3_), channel_id=1, source_target_pairs={{0,28},{4,0},{8,4},{12,8},{16,12},{20,16},{24,20},{28,24},{32,60},... | collective-permute-start | bytes 1572872 | tf_op jit(solution)/shard_map/ppermute | solution.py:32
  63.4 2.9 %lists.1.refs_0_.list_ref = s32[195]{0:T(256)} custom-call(s32[1]{0:T(128)} %bitcast.1.at_ref, s32[128]{0:T(128)} %order_ref.1, s32[128,128]{1,0:T(8,128)} %table_ref.1), custom_call_target="tpu_custom_call" | custom-call | tf_op jit(solution)/shard_map/lists/pallas_call | solution.py:84
  66.3 0.0 all-to-all-done.refs_1_
  66.3 0.0 copy-start.5
  66.3 1.0 copy-done.5
  67.4 0.0 copy-start.10
  67.4 0.7 copy-done.10
  68.1 0.0 copy-start.13
  68.1 1.0 copy-done.13
  69.1 5.3 %shard_map.56 = (f32[3,8,128,256]{3,2,1,0:T(8,128)S(1)}, f32[3,8,128,128]{3,2,1,0:T(8,128)S(1)}) custom-call(s32[195]{0:T(256)S(1)} %copy-done.10, bf16[4,128,1024]{2,1,0:T(8,128)(2,1)S(1)} %all-to-all-done.refs_1_, bf16[4,256,256]{2,1,0:T(8,128)(2,1)S(1)} %copy-done.5, bf16[4,256,256]{2,1,0:T(8,128)(2,1)S(1)} %copy-done.13, ...), custom_call_target="tpu_custom_call" | custom-call | flops 2415919104 | bytes 4194304 | tf_op jit(solution)/shard_map/pallas_call | solution.py:209
  74.4 0.0 collective-permute-done.4.refs_7_.refs_2_
  74.4 1.9 %collective-permute-start.6 = (bf16[2,256,256]{2,1,0:T(8,128)(2,1)S(1)}, bf16[2,256,256]{2,1,0:T(8,128)(2,1)S(1)}, u32[]{:S(2)}, u32[]{:S(2)}) collective-permute-start(bf16[2,256,256]{2,1,0:T(8,128)(2,1)S(1)} %slice.17), channel_id=1, source_target_pairs={{0,4},{4,8},{8,12},{12,16},{16,20},{20,24},{24,28},{28,0},{32,36},... | collective-permute-start | bytes 786440 | tf_op jit(solution)/shard_map/ppermute | solution.py:32
  76.3 0.0 copy-done.2
  76.4 2.9 %shard_map.57 = (f32[3,8,128,256]{3,2,1,0:T(8,128)S(1)}, f32[3,8,128,128]{3,2,1,0:T(8,128)S(1)}) custom-call(s32[195]{0:T(256)S(1)} %copy-done.10, bf16[4,128,1024]{2,1,0:T(8,128)(2,1)S(1)} %all-to-all-done.refs_1_, bf16[4,256,256]{2,1,0:T(8,128)(2,1)S(1)} %collective-permute-done.2.refs_5_.refs_2_, ...), custom_call_target="tpu_custom_call" | custom-call | flops 1610612736 | bytes 4194304 | tf_op jit(solution)/shard_map/pallas_call | solution.py:209
  79.2 0.0 collective-permute-done.5.refs_8_.refs_3_
  79.3 5.5 %collective-permute-start.7 = (bf16[2,256,256]{2,1,0:T(8,128)(2,1)S(1)}, bf16[2,256,256]{2,1,0:T(8,128)(2,1)S(1)}, u32[]{:S(2)}, u32[]{:S(2)}) collective-permute-start(bf16[2,256,256]{2,1,0:T(8,128)(2,1)S(1)} %slice.18), channel_id=1, source_target_pairs={{0,28},{4,0},{8,4},{12,8},{16,12},{20,16},{24,20},{28,24},{32,60},... | collective-permute-start | bytes 786440 | tf_op jit(solution)/shard_map/ppermute | solution.py:32
  84.8 2.9 %shard_map.58 = (f32[3,8,128,256]{3,2,1,0:T(8,128)S(1)}, f32[3,8,128,128]{3,2,1,0:T(8,128)S(1)}) custom-call(s32[195]{0:T(256)S(1)} %copy-done.10, bf16[4,128,1024]{2,1,0:T(8,128)(2,1)S(1)} %all-to-all-done.refs_1_, bf16[4,256,256]{2,1,0:T(8,128)(2,1)S(1)} %collective-permute-done.4.refs_7_.refs_2_, ...), custom_call_target="tpu_custom_call" | custom-call | flops 1610612736 | bytes 4194304 | tf_op jit(solution)/shard_map/pallas_call | solution.py:209
  87.7 0.0 collective-permute-done.6
  87.7 0.4 collective-permute-done.7
  88.1 5.1 %shard_map.59 = bf16[4,128,1152]{2,1,0:T(8,128)(2,1)} custom-call(s32[195]{0:T(256)S(1)} %copy-done.10, bf16[4,128,1024]{2,1,0:T(8,128)(2,1)S(1)} %all-to-all-done.refs_1_, bf16[4,256,256]{2,1,0:T(8,128)(2,1)S(1)} %constant_dynamic-update-slice_fusion.refs_9_.refs_2_, f32[3,8,128,256]{3,2,1,0:T(8,128)S(1)} %get-tuple-element.17.refs_3_, ...), custom_call_target="tpu_custom_call" | custom-call | flops 805306368 | bytes 4194304 | tf_op jit(solution)/shard_map/pallas_call | solution.py:209
  93.2 0.0 copy-start.9
  93.2 0.0 copy-start.11
  93.2 7.8 %all-to-all-start.1 = ((bf16[4,128,1152]{2,1,0:T(8,128)(2,1)}), bf16[4,128,1152]{2,1,0:T(8,128)(2,1)S(1)}, u32[]{:S(2)}, u32[]{:S(2)}) async-start(bf16[4,128,1152]{2,1,0:T(8,128)(2,1)} %shard_map.59), calls=%async_computation.1 | async-start | bytes 2359296 | tf_op jit(solution)/shard_map/all_to_all | solution.py:40
  101.0 0.0 copy-done.9
  101.0 0.0 copy-done.11
  101.0 0.0 copy-start.3
  101.0 1.0 copy-done.3
  102.1 0.0 copy-start.6
  102.1 1.0 copy-done.6
  103.1 0.0 copy-start.14
  103.1 1.0 copy-done.14
  104.2 6.6 %shard_map.55.own_ref = bf16[1,128,1152]{2,1,0:T(8,128)(2,1)S(1)} custom-call(s32[195]{0:T(256)S(1)} %copy-done.11, bf16[1,128,1024]{2,1,0:T(8,128)(2,1)S(1)} %bitcast.12, bf16[4,256,256]{2,1,0:T(8,128)(2,1)S(1)} %copy-done.6, bf16[4,256,256]{2,1,0:T(8,128)(2,1)S(1)} %copy-done.14, bf16[4,256,256]{2,1,0:T(8,128)(2,1)} %collective-permute-done.1.refs_4_, ...), custom_call_target="tpu_custom_call" | custom-call | flops 2147483648 | bytes 4194304 | tf_op jit(solution)/shard_map/pallas_call | solution.py:209
  110.7 0.0 copy-start.7
  110.7 0.7 copy-done.7
  111.4 0.3 all-to-all-done.1.part_ref
  111.7 0.0 copy-start
  111.7 2.2 %copy-done = bf16[1024,2048]{1,0:T(8,128)(2,1)S(1)} copy-done((bf16[1024,2048]{1,0:T(8,128)(2,1)S(1)}, bf16[1024,2048]{1,0:T(8,128)(2,1)}, u32[]{:S(2)}) %copy-start) | copy-done | bytes 4194328
  113.9 1.0 copy-done.8
  114.9 1.8 %shard_map.60 = (bf16[128,1024]{1,0:T(8,128)(2,1)S(1)}, bf16[2,128,512]{2,1,0:T(8,128)(2,1)S(1)}) custom-call(s32[1]{0:T(128)} %bitcast.at_ref, s32[195]{0:T(256)S(1)} %copy-done.11, bf16[1,128,1152]{2,1,0:T(8,128)(2,1)S(1)} %copy-done.8, bf16[4,128,1152]{2,1,0:T(8,128)(2,1)S(1)} %all-to-all-done.1.part_ref, bf16[1024,2048]{1,0:T(8,128)(2,1)S(1)} %copy-done), custom_call_target="tpu_custom_call" | custom-call | flops 268435456 | bytes 5242880 | tf_op jit(solution)/shard_map/pallas_call | solution.py:258
  116.7 8.6 %collective-permute-start.8 = (bf16[2,128,512]{2,1,0:T(8,128)(2,1)S(1)}, bf16[2,128,512]{2,1,0:T(8,128)(2,1)S(1)}, u32[]{:S(2)}, u32[]{:S(2)}) collective-permute-start(bf16[2,128,512]{2,1,0:T(8,128)(2,1)S(1)} %get-tuple-element.20), channel_id=1, source_target_pairs={{0,1},{1,0},{2,3},{3,2},{4,5},{5,4},{6,7},{7,6},{8,9},{9,8},{10,11... | collective-permute-start | bytes 786440 | tf_op jit(solution)/shard_map/ppermute | solution.py:296
  125.4 0.0 copy-done.1
  125.4 0.5 shard_map.61
  125.9 0.7 collective-permute-done.8
  126.5 0.1 convert_add_fusion
  126.6 6.0 %collective-permute-start.9 = (bf16[128,512]{1,0:T(8,128)(2,1)S(1)}, bf16[128,512]{1,0:T(8,128)(2,1)S(1)}, u32[]{:S(2)}, u32[]{:S(2)}) collective-permute-start(bf16[128,512]{1,0:T(8,128)(2,1)S(1)} %fusion.2), channel_id=1, source_target_pairs={{0,2},{1,3},{2,0},{3,1},{4,6},{5,7},{6,4},{7,5},{8,10},{9,11},{10,... | collective-permute-start | bytes 393224 | tf_op jit(solution)/shard_map/ppermute | solution.py:304
  132.7 3.5 %collective-permute-done.9 = bf16[128,512]{1,0:T(8,128)(2,1)S(1)} collective-permute-done((bf16[128,512]{1,0:T(8,128)(2,1)S(1)}, bf16[128,512]{1,0:T(8,128)(2,1)S(1)}, u32[]{:S(2)}, u32[]{:S(2)}) %collective-permute-start.9) | collective-permute-done | bytes 131104 | tf_op jit(solution)/shard_map/ppermute | solution.py:304
  136.2 0.7 fusion.1
  (7 shorter events, 0.1 us)
Async XLA Ops:
  21.5 19.5 %copy-start.4 = (bf16[4,256,256]{2,1,0:T(8,128)(2,1)}, bf16[4,256,256]{2,1,0:T(8,128)(2,1)S(1)}, u32[]{:S(2)}) copy-start(bf16[4,256,256]{2,1,0:T(8,128)(2,1)S(1)} %all_gather.3.refs_2_) | copy-start | bytes 1572868
  21.5 15.5 %collective-permute-start = (bf16[4,256,256]{2,1,0:T(8,128)(2,1)S(1)}, bf16[4,256,256]{2,1,0:T(8,128)(2,1)S(1)}, u32[]{:S(2)}, u32[]{:S(2)}) collective-permute-start(bf16[4,256,256]{2,1,0:T(8,128)(2,1)S(1)} %all_gather.3.refs_2_), channel_id=1, source_target_pairs={{0,4},{4,8},{8,12},{12,16},{16,20},{20,24},{24,28},{28,0},{32,36},... | collective-permute-start | bytes 1572872 | tf_op jit(solution)/shard_map/ppermute | solution.py:32
  24.7 20.3 %collective-permute-start.1 = (bf16[4,256,256]{2,1,0:T(8,128)(2,1)S(1)}, bf16[4,256,256]{2,1,0:T(8,128)(2,1)}, u32[]{:S(2)}, u32[]{:S(2)}) collective-permute-start(bf16[4,256,256]{2,1,0:T(8,128)(2,1)S(1)} %all_gather.3.refs_2_), channel_id=1, source_target_pairs={{0,28},{4,0},{8,4},{12,8},{16,12},{20,16},{24,20},{28,24},{32,60},... | collective-permute-start | bytes 1572872 | tf_op jit(solution)/shard_map/ppermute | solution.py:32
  37.0 4.0 %copy-start.12 = (bf16[4,256,256]{2,1,0:T(8,128)(2,1)}, bf16[4,256,256]{2,1,0:T(8,128)(2,1)S(1)}, u32[]{:S(2)}) copy-start(bf16[4,256,256]{2,1,0:T(8,128)(2,1)S(1)} %collective-permute-done.refs_3_) | copy-start | bytes 1572868
  37.0 14.1 %collective-permute-start.2 = (bf16[4,256,256]{2,1,0:T(8,128)(2,1)S(1)}, bf16[4,256,256]{2,1,0:T(8,128)(2,1)S(1)}, u32[]{:S(2)}, u32[]{:S(2)}) collective-permute-start(bf16[4,256,256]{2,1,0:T(8,128)(2,1)S(1)} %collective-permute-done.refs_3_), channel_id=1, source_target_pairs={{0,4},{4,8},{8,12},{12,16},{16,20},{20,24},{24,28},{28,0},{32,36},... | collective-permute-start | bytes 1572872 | tf_op jit(solution)/shard_map/ppermute | solution.py:32
  41.0 25.3 %all-to-all-start = ((bf16[4,128,1024]{2,1,0:T(8,128)(2,1)}), bf16[4,128,1024]{2,1,0:T(8,128)(2,1)S(1)}, u32[]{:S(2)}, u32[]{:S(2)}) async-start(bf16[4,128,1024]{2,1,0:T(8,128)(2,1)} %broadcast_in_dim.10), calls=%async_computation | async-start | bytes 2097152 | tf_op jit(solution)/shard_map/all_to_all | solution.py:40
  45.0 13.1 %collective-permute-start.3 = (bf16[4,256,256]{2,1,0:T(8,128)(2,1)}, bf16[4,256,256]{2,1,0:T(8,128)(2,1)S(1)}, u32[]{:S(2)}, u32[]{:S(2)}) collective-permute-start(bf16[4,256,256]{2,1,0:T(8,128)(2,1)} %collective-permute-done.1.refs_4_), channel_id=1, source_target_pairs={{0,28},{4,0},{8,4},{12,8},{16,12},{20,16},{24,20},{28,24},{32,60},... | collective-permute-start | bytes 1572872 | tf_op jit(solution)/shard_map/ppermute | solution.py:32
  51.1 23.2 %collective-permute-start.4 = (bf16[4,256,256]{2,1,0:T(8,128)(2,1)S(1)}, bf16[4,256,256]{2,1,0:T(8,128)(2,1)S(1)}, u32[]{:S(2)}, u32[]{:S(2)}) collective-permute-start(bf16[4,256,256]{2,1,0:T(8,128)(2,1)S(1)} %collective-permute-done.2.refs_5_.refs_2_), channel_id=1, source_target_pairs={{0,4},{4,8},{8,12},{12,16},{16,20},{20,24},{24,28},{28,0},{32,36},... | collective-permute-start | bytes 1572872 | tf_op jit(solution)/shard_map/ppermute | solution.py:32
  58.2 18.2 %copy-start.2 = (bf16[4,256,256]{2,1,0:T(8,128)(2,1)}, bf16[4,256,256]{2,1,0:T(8,128)(2,1)S(1)}, u32[]{:S(2)}) copy-start(bf16[4,256,256]{2,1,0:T(8,128)(2,1)S(1)} %collective-permute-done.3.refs_6_.refs_3_) | copy-start | bytes 1572868
  58.2 21.1 %collective-permute-start.5 = (bf16[4,256,256]{2,1,0:T(8,128)(2,1)S(1)}, bf16[4,256,256]{2,1,0:T(8,128)(2,1)S(1)}, u32[]{:S(2)}, u32[]{:S(2)}) collective-permute-start(bf16[4,256,256]{2,1,0:T(8,128)(2,1)S(1)} %collective-permute-done.3.refs_6_.refs_3_), channel_id=1, source_target_pairs={{0,28},{4,0},{8,4},{12,8},{16,12},{20,16},{24,20},{28,24},{32,60},... | collective-permute-start | bytes 1572872 | tf_op jit(solution)/shard_map/ppermute | solution.py:32
  66.3 1.0 copy-start.5
  67.4 0.7 copy-start.10
  68.1 1.0 copy-start.13
  74.4 13.2 %collective-permute-start.6 = (bf16[2,256,256]{2,1,0:T(8,128)(2,1)S(1)}, bf16[2,256,256]{2,1,0:T(8,128)(2,1)S(1)}, u32[]{:S(2)}, u32[]{:S(2)}) collective-permute-start(bf16[2,256,256]{2,1,0:T(8,128)(2,1)S(1)} %slice.17), channel_id=1, source_target_pairs={{0,4},{4,8},{8,12},{12,16},{16,20},{20,24},{24,28},{28,0},{32,36},... | collective-permute-start | bytes 786440 | tf_op jit(solution)/shard_map/ppermute | solution.py:32
  79.3 8.8 %collective-permute-start.7 = (bf16[2,256,256]{2,1,0:T(8,128)(2,1)S(1)}, bf16[2,256,256]{2,1,0:T(8,128)(2,1)S(1)}, u32[]{:S(2)}, u32[]{:S(2)}) collective-permute-start(bf16[2,256,256]{2,1,0:T(8,128)(2,1)S(1)} %slice.18), channel_id=1, source_target_pairs={{0,28},{4,0},{8,4},{12,8},{16,12},{20,16},{24,20},{28,24},{32,60},... | collective-permute-start | bytes 786440 | tf_op jit(solution)/shard_map/ppermute | solution.py:32
  93.2 7.8 %copy-start.9 = (bf16[128,1024]{1,0:T(8,128)(2,1)S(1)}, bf16[128,1024]{1,0:T(8,128)(2,1)}, u32[]{:S(2)}) copy-start(bf16[128,1024]{1,0:T(8,128)(2,1)} %param.5) | copy-start | bytes 786436
  93.2 7.8 %copy-start.11 = (s32[195]{0:T(256)S(1)}, s32[195]{0:T(256)}, u32[]{:S(2)}) copy-start(s32[195]{0:T(256)} %lists.1.refs_0_.list_ref) | copy-start | bytes 2344
  93.2 18.5 %all-to-all-start.1 = ((bf16[4,128,1152]{2,1,0:T(8,128)(2,1)}), bf16[4,128,1152]{2,1,0:T(8,128)(2,1)S(1)}, u32[]{:S(2)}, u32[]{:S(2)}) async-start(bf16[4,128,1152]{2,1,0:T(8,128)(2,1)} %shard_map.59), calls=%async_computation.1 | async-start | bytes 2359296 | tf_op jit(solution)/shard_map/all_to_all | solution.py:40
  101.0 1.0 copy-start.3
  102.1 1.0 copy-start.6
  103.1 1.0 copy-start.14
  110.7 0.7 copy-start.7
  111.7 2.2 %copy-start = (bf16[1024,2048]{1,0:T(8,128)(2,1)S(1)}, bf16[1024,2048]{1,0:T(8,128)(2,1)}, u32[]{:S(2)}) copy-start(bf16[1024,2048]{1,0:T(8,128)(2,1)} %w_ref.3) | copy-start | bytes 12582916
  113.9 1.0 copy-start.8
  114.9 10.5 %copy-start.1 = (bf16[1024,2048]{1,0:T(8,128)(2,1)S(1)}, bf16[1024,2048]{1,0:T(8,128)(2,1)}, u32[]{:S(2)}) copy-start(bf16[1024,2048]{1,0:T(8,128)(2,1)} %w_ref.3) | copy-start | bytes 12582916
  116.7 9.8 %collective-permute-start.8 = (bf16[2,128,512]{2,1,0:T(8,128)(2,1)S(1)}, bf16[2,128,512]{2,1,0:T(8,128)(2,1)S(1)}, u32[]{:S(2)}, u32[]{:S(2)}) collective-permute-start(bf16[2,128,512]{2,1,0:T(8,128)(2,1)S(1)} %get-tuple-element.20), channel_id=1, source_target_pairs={{0,1},{1,0},{2,3},{3,2},{4,5},{5,4},{6,7},{7,6},{8,9},{9,8},{10,11... | collective-permute-start | bytes 786440 | tf_op jit(solution)/shard_map/ppermute | solution.py:296
  126.6 9.5 %collective-permute-start.9 = (bf16[128,512]{1,0:T(8,128)(2,1)S(1)}, bf16[128,512]{1,0:T(8,128)(2,1)S(1)}, u32[]{:S(2)}, u32[]{:S(2)}) collective-permute-start(bf16[128,512]{1,0:T(8,128)(2,1)S(1)} %fusion.2), channel_id=1, source_target_pairs={{0,2},{1,3},{2,0},{3,1},{4,6},{5,7},{6,4},{7,5},{8,10},{9,11},{10,... | collective-permute-start | bytes 393224 | tf_op jit(solution)/shard_map/ppermute | solution.py:304
where the time goes:
time: 138 us; the launch traced here: 137 us
  starting transfers between devices  54.5 us (39%)
  Pallas kernels  27.9 us (20%)
  blocking collectives  21.5 us (16%)
  waiting for transfers between devices  20 us (14%)
  local copies, waits for them, and re-layouts  11.9 us (9%)
    ppermute x8, starting transfers between devices, _shift(): return lax.ppermute(a, 'seq', pairs)  28 us
    pallas_call x5, Pallas kernels, _attend(): pl.pallas_call(functools.partial(_attend_kernel, name=name, first=first,...  22.7 us
    all_gather x1, blocking collectives, per_device(): lax.all_gather(kv, 'seq', axis=0, tiled=True, axis_index_groups=Z_GROUPS)  21.5 us
    ppermute x8, waiting for transfers between devices, _shift(): return lax.ppermute(a, 'seq', pairs)  15.5 us
    all_to_all x2, starting transfers between devices, _swap(): return lax.all_to_all(a, 'seq', 0, 0, tiled=True, axis_index_groups=groups)  11.8 us
    unnamed x31, local copies, waits for them, and re-layouts  9.77 us
    ppermute x1, starting transfers between devices, per_device(): took = lax.ppermute(give, 'tp', [(t, t ^ 1) for t in range(4)])  8.63 us
    ppermute x1, starting transfers between devices, per_device(): lax.ppermute(both[1].astype(jnp.bfloat16), 'tp', [(t, t ^ 2) for t in ran...  6.04 us
  transfers between devices with their start and end apart: 12, of which 7 were waited for; matrix products, arithmetic and copies ran while one was open for 2% of the time, Pallas kernels for 15%

commit v1 on v0

--- a/solution.py
+++ b/solution.py
@@ -46,7 +46,8 @@
     "att2": (OTHERS, (6, 2)),
     "att3": (OTHERS, (5, 3)),
     "att4": (OTHERS, (4,)),
-    "att_own": ((0,), (0, 7, 1, 6, 2, 5, 3, 4)),
+    "own1": ((0,), (0, 7, 1)),
+    "own2": ((0,), (6, 2, 5, 3, 4)),
 }
 PLACES = {}
 LIST_END = 2
@@ -64,16 +65,20 @@
     out_ref[0] = x
     out_ref[1] = z
     keys = {(d, n): order_ref[x * 32 + n * 8 + ((y + d) & 7)] for d in range(NY) for n in range(NZ)}
-    for name, (queries, dists) in CALLS.items():
-        for j, from_x in enumerate(queries):
-            mine = order_ref[((x + from_x) & 3) * 32 + z * 8 + y]
-            place = PLACES[name, j]
+    for from_x in range(NX):
+        mine = order_ref[((x + from_x) & 3) * 32 + z * 8 + y]
+        seen = {
+            at: jnp.where((key < mine) & (table_ref[mine, key] == 1), 1, 0) for at, key in keys.items()
+        }
+        for name, (queries, dists) in CALLS.items():
+            if from_x not in queries:
+                continue
+            place = PLACES[name, queries.index(from_x)]
             count = jnp.int32(0)
             for c, d in enumerate(dists):
                 for n in range(NZ):
-                    key = keys[d, n]
                     out_ref[place + 1 + count] = c * NZ + n
-                    count += jnp.where((key < mine) & (table_ref[mine, key] == 1), 1, 0)
+                    count += seen[d, n]
             for n in range(KEYS - 1):
                 out_ref[place + 1 + count + n] = 0
             out_ref[place] = count
@@ -158,7 +163,7 @@
     else:
         acc_ref[...] = state[0][...]
         m_ref[...] = state[1][...]
-    if own:
+    if own and dists[0] == 0:
         key = lax.broadcasted_iota(jnp.int32, (ROWS, ROWS), 1)
         row = lax.broadcasted_iota(jnp.int32, (ROWS, ROWS), 0)
         bias = jnp.concatenate([jnp.where(key > row, NEG, 0.0)] * 4, axis=0)
@@ -220,12 +225,12 @@
     return got[0] if last else got
 
 
-def _combine_kernel(at_ref, list_ref, own_ref, part_ref, w_ref, att_ref, out_ref):
+def _combine_kernel(at_ref, list_ref, own1_ref, own2_ref, part_ref, w_ref, att_ref, out_ref):
     x = list_ref[0]
+    sources = [(own1_ref, 0), (own2_ref, 0)] + [(part_ref, (x + j) & 3) for j in range(1, NX)]
     lses = []
-    for j in range(NX):
-        ext = own_ref[0, :, 8 * HEAD :] if j == 0 else part_ref[(x + j) & 3, :, 8 * HEAD :]
-        ext = ext.astype(jnp.float32)
+    for ref, i in sources:
+        ext = ref[i, :, 8 * HEAD :].astype(jnp.float32)
         lses.append(ext[:, 0:8] + ext[:, 8:16] + ext[:, 16:24])
     top = functools.reduce(jnp.maximum, lses)
     ws = [jnp.exp2(v - top) for v in lses]
@@ -233,9 +238,9 @@
     ws = [w / total for w in ws]
     for h in range(8):
         at = slice(h * HEAD, (h + 1) * HEAD)
-        mixed = ws[0][:, h : h + 1] * own_ref[0, :, at].astype(jnp.float32)
-        for j in range(1, NX):
-            mixed += ws[j][:, h : h + 1] * part_ref[(x + j) & 3, :, at].astype(jnp.float32)
+        mixed = jnp.zeros((ROWS, HEAD), jnp.float32)
+        for w, (ref, i) in zip(ws, sources):
+            mixed += w[:, h : h + 1] * ref[i, :, at].astype(jnp.float32)
         att_ref[:, at] = mixed.astype(jnp.bfloat16)
     _columns(at_ref, att_ref, w_ref, out_ref, 1)
 
@@ -277,6 +282,7 @@
     f1, b1 = _ring(near, 1), _ring(near, -1)
     f2, b2 = _ring(f1, 1), _ring(b1, -1)
     state = _attend("att1", lists, q, [near, f1, b1], None, False)
+    own1 = _attend("own1", lists, queries[None], [near, f1, b1], None, True)
     f3, b3 = _ring(f2, 1), _ring(b2, -1)
     state = _attend("att2", lists, q, [f2, b2], state, False)
     f4, b4 = _ring(f3[:2], 1), _ring(b3[2:], -1)
@@ -284,21 +290,17 @@
     far = jnp.concatenate([f4, b4], axis=0)
     parts = _attend("att4", lists, q, [far], state, True)
     parts = _swap(parts, X_GROUPS)
-    chunks = [near, f1, b1, f2, b2, f3, b3, far]
-    own = _attend("att_own", lists, queries[None], chunks, None, True)
+    own2 = _attend("own2", lists, queries[None], [f2, b2, f3, b3, far], None, True)
     me = lax.axis_index("tp").astype(jnp.int32).reshape(1)
     att, give = _call(
         _combine_kernel,
-        [me, lists, own, parts, proj_weight],
+        [me, lists, own1, own2, parts, proj_weight],
         (jax.ShapeDtypeStruct((ROWS, 8 * HEAD), jnp.bfloat16), jax.ShapeDtypeStruct((2, ROWS, 512), jnp.bfloat16)),
         2 * ROWS * 1024 * 1024,
     )
     took = lax.ppermute(give, "tp", [(t, t ^ 1) for t in range(4)])
     keep = _call(
-        _keep_kernel,
-        [me, att, proj_weight],
-        jax.ShapeDtypeStruct((2, ROWS, 512), jnp.float32),
-        2 * ROWS * 1024 * 1024,
+        _keep_kernel, [me, att, proj_weight], jax.ShapeDtypeStruct((2, ROWS, 512), jnp.float32), 2 * ROWS * 1024 * 1024
     )
     both = keep + took.astype(jnp.float32)
     beside = lax.ppermute(both[1].astype(jnp.bfloat16), "tp", [(t, t ^ 2) for t in range(4)])

time: 138 us -> 140 us (1.014)
    pallas_call x5 -> x6, Pallas kernels: 22.7 us -> 23.5 us  [_attend(): pl.pallas_call(functools.partial(_attend_kernel, name=name, first=first,...]
    unnamed x31 -> x35, local copies, waits for them, and re-layouts: 9.77 us -> 10.5 us
  transfers between devices with their start and end apart: 12 -> 12, of which waited for: 7 -> 6; matrix products, arithmetic and copies ran while one was open for 2% -> 2% of each run, Pallas kernels for 15% -> 16%
where the time goes in v1:
time: 140 us; the launch traced here: 138 us
  starting transfers between devices  54.2 us (39%)
  Pallas kernels  29 us (21%)
  blocking collectives  21.5 us (15%)
  waiting for transfers between devices  19.7 us (14%)
  local copies, waits for them, and re-layouts  12.6 us (9%)
    ppermute x8, starting transfers between devices, _shift(): return lax.ppermute(a, 'seq', pairs)  28 us
    pallas_call x6, Pallas kernels, _attend(): pl.pallas_call(functools.partial(_attend_kernel, name=name, first=first,...  23.5 us
    all_gather x1, blocking collectives, per_device(): lax.all_gather(kv, 'seq', axis=0, tiled=True, axis_index_groups=Z_GROUPS)  21.5 us
    ppermute x8, waiting for transfers between devices, _shift(): return lax.ppermute(a, 'seq', pairs)  15.5 us
    all_to_all x2, starting transfers between devices, _swap(): return lax.all_to_all(a, 'seq', 0, 0, tiled=True, axis_index_groups=groups)  11.8 us
    unnamed x35, local copies, waits for them, and re-layouts  10.5 us
    ppermute x1, starting transfers between devices, per_device(): took = lax.ppermute(give, 'tp', [(t, t ^ 1) for t in range(4)])  8.34 us
    ppermute x1, starting transfers between devices, per_device(): lax.ppermute(both[1].astype(jnp.bfloat16), 'tp', [(t, t ^ 2) for t in ran...  6.05 us
  transfers between devices with their start and end apart: 12, of which 6 were waited for; matrix products, arithmetic and copies ran while one was open for 2% of the time, Pallas kernels for 16%

profile of v1, /device:TPU:1, one launch (start us, length us, event | category | flops | bytes accessed | tf_op | source)
XLA Modules:
  0.0 138.1 jit_solution(14089293281224378958)
XLA Ops:
  0.0 21.5 %all_gather.3.refs_2_ = bf16[4,256,256]{2,1,0:T(8,128)(2,1)S(1)} all-gather(bf16[1,256,256]{2,1,0:T(8,128)(2,1)} %bitcast.14), channel_id=1, replica_groups={{0,32,64,96},{4,36,68,100},{8,40,72,104},{12,44,76,108},{16,48,80,112},..., dimensions={0}, use_global_device_ids=true | all-gather | bytes 655360 | tf_op jit(solution)/shard_map/all_gather | solution.py:279
  21.5 0.0 copy-start.4
  21.5 3.2 %collective-permute-start = (bf16[4,256,256]{2,1,0:T(8,128)(2,1)S(1)}, bf16[4,256,256]{2,1,0:T(8,128)(2,1)S(1)}, u32[]{:S(2)}, u32[]{:S(2)}) collective-permute-start(bf16[4,256,256]{2,1,0:T(8,128)(2,1)S(1)} %all_gather.3.refs_2_), channel_id=1, source_target_pairs={{0,4},{4,8},{8,12},{12,16},{16,20},{20,24},{24,28},{28,0},{32,36},... | collective-permute-start | bytes 1572872 | tf_op jit(solution)/shard_map/ppermute | solution.py:32
  24.7 3.8 %collective-permute-start.1 = (bf16[4,256,256]{2,1,0:T(8,128)(2,1)S(1)}, bf16[4,256,256]{2,1,0:T(8,128)(2,1)}, u32[]{:S(2)}, u32[]{:S(2)}) collective-permute-start(bf16[4,256,256]{2,1,0:T(8,128)(2,1)S(1)} %all_gather.3.refs_2_), channel_id=1, source_target_pairs={{0,28},{4,0},{8,4},{12,8},{16,12},{20,16},{24,20},{28,24},{32,60},... | collective-permute-start | bytes 1572872 | tf_op jit(solution)/shard_map/ppermute | solution.py:32
  28.5 8.5 %collective-permute-done.refs_3_ = bf16[4,256,256]{2,1,0:T(8,128)(2,1)S(1)} collective-permute-done((bf16[4,256,256]{2,1,0:T(8,128)(2,1)S(1)}, bf16[4,256,256]{2,1,0:T(8,128)(2,1)S(1)}, u32[]{:S(2)}, u32[]{:S(2)}) %collective-permute-start) | collective-permute-done | bytes 524320 | tf_op jit(solution)/shard_map/ppermute | solution.py:32
  37.0 0.0 copy-start.14
  37.0 1.9 %collective-permute-start.2 = (bf16[4,256,256]{2,1,0:T(8,128)(2,1)S(1)}, bf16[4,256,256]{2,1,0:T(8,128)(2,1)S(1)}, u32[]{:S(2)}, u32[]{:S(2)}) collective-permute-start(bf16[4,256,256]{2,1,0:T(8,128)(2,1)S(1)} %collective-permute-done.refs_3_), channel_id=1, source_target_pairs={{0,4},{4,8},{8,12},{12,16},{16,20},{20,24},{24,28},{28,0},{32,36},... | collective-permute-start | bytes 1572872 | tf_op jit(solution)/shard_map/ppermute | solution.py:32
  38.9 2.1 %broadcast_in_dim.5 = bf16[4,128,1024]{2,1,0:T(8,128)(2,1)} broadcast(bf16[128,1024]{1,0:T(8,128)(2,1)} %param.5), dimensions={1,2} | broadcast | bytes 1310720 | tf_op jit(solution)/shard_map/broadcast_in_dim | solution.py:280
  41.0 0.0 copy-done.4
  41.0 0.0 copy-done.14
  41.0 4.0 %all-to-all-start = ((bf16[4,128,1024]{2,1,0:T(8,128)(2,1)}), bf16[4,128,1024]{2,1,0:T(8,128)(2,1)S(1)}, u32[]{:S(2)}, u32[]{:S(2)}) async-start(bf16[4,128,1024]{2,1,0:T(8,128)(2,1)} %broadcast_in_dim.5), calls=%async_computation | async-start | bytes 2097152 | tf_op jit(solution)/shard_map/all_to_all | solution.py:40
  45.0 0.0 collective-permute-done.1.refs_4_
  45.0 4.6 %collective-permute-start.3 = (bf16[4,256,256]{2,1,0:T(8,128)(2,1)}, bf16[4,256,256]{2,1,0:T(8,128)(2,1)S(1)}, u32[]{:S(2)}, u32[]{:S(2)}) collective-permute-start(bf16[4,256,256]{2,1,0:T(8,128)(2,1)} %collective-permute-done.1.refs_4_), channel_id=1, source_target_pairs={{0,28},{4,0},{8,4},{12,8},{16,12},{20,16},{24,20},{28,24},{32,60},... | collective-permute-start | bytes 1572872 | tf_op jit(solution)/shard_map/ppermute | solution.py:32
  49.6 1.5 %collective-permute-done.2.refs_2_ = bf16[4,256,256]{2,1,0:T(8,128)(2,1)S(1)} collective-permute-done((bf16[4,256,256]{2,1,0:T(8,128)(2,1)S(1)}, bf16[4,256,256]{2,1,0:T(8,128)(2,1)S(1)}, u32[]{:S(2)}, u32[]{:S(2)}) %collective-permute-start.2) | collective-permute-done | bytes 524320 | tf_op jit(solution)/shard_map/ppermute | solution.py:32
  51.1 1.9 %collective-permute-start.4 = (bf16[4,256,256]{2,1,0:T(8,128)(2,1)S(1)}, bf16[4,256,256]{2,1,0:T(8,128)(2,1)S(1)}, u32[]{:S(2)}, u32[]{:S(2)}) collective-permute-start(bf16[4,256,256]{2,1,0:T(8,128)(2,1)S(1)} %collective-permute-done.2.refs_2_), channel_id=1, source_target_pairs={{0,4},{4,8},{8,12},{12,16},{16,20},{20,24},{24,28},{28,0},{32,36},... | collective-permute-start | bytes 1572872 | tf_op jit(solution)/shard_map/ppermute | solution.py:32
  53.1 5.1 %collective-permute-done.3.refs_3_ = bf16[4,256,256]{2,1,0:T(8,128)(2,1)S(1)} collective-permute-done((bf16[4,256,256]{2,1,0:T(8,128)(2,1)}, bf16[4,256,256]{2,1,0:T(8,128)(2,1)S(1)}, u32[]{:S(2)}, u32[]{:S(2)}) %collective-permute-start.3) | collective-permute-done | bytes 524320 | tf_op jit(solution)/shard_map/ppermute | solution.py:32
  58.2 0.0 copy-start.2
  58.2 5.2 %collective-permute-start.5 = (bf16[4,256,256]{2,1,0:T(8,128)(2,1)S(1)}, bf16[4,256,256]{2,1,0:T(8,128)(2,1)S(1)}, u32[]{:S(2)}, u32[]{:S(2)}) collective-permute-start(bf16[4,256,256]{2,1,0:T(8,128)(2,1)S(1)} %collective-permute-done.3.refs_3_), channel_id=1, source_target_pairs={{0,28},{4,0},{8,4},{12,8},{16,12},{20,16},{24,20},{28,24},{32,60},... | collective-permute-start | bytes 1572872 | tf_op jit(solution)/shard_map/ppermute | solution.py:32
  63.4 3.1 %lists.1.refs_0_.list_ref = s32[200]{0:T(256)} custom-call(s32[1]{0:T(128)} %bitcast.1.at_ref, s32[128]{0:T(128)} %order_ref.1, s32[128,128]{1,0:T(8,128)} %table_ref.1), custom_call_target="tpu_custom_call" | custom-call | tf_op jit(solution)/shard_map/lists/pallas_call | solution.py:89
  66.4 0.0 all-to-all-done.refs_1_
  66.5 0.0 copy-start.5
  66.5 1.0 copy-done.5
  67.5 0.0 copy-start.12
  67.5 0.7 copy-done.12
  68.2 0.0 copy-start.15
  68.2 1.0 copy-done.15
  69.2 5.3 %shard_map.57 = (f32[3,8,128,256]{3,2,1,0:T(8,128)S(1)}, f32[3,8,128,128]{3,2,1,0:T(8,128)S(1)}) custom-call(s32[200]{0:T(256)S(1)} %copy-done.12, bf16[4,128,1024]{2,1,0:T(8,128)(2,1)S(1)} %all-to-all-done.refs_1_, bf16[4,256,256]{2,1,0:T(8,128)(2,1)S(1)} %copy-done.5, bf16[4,256,256]{2,1,0:T(8,128)(2,1)S(1)} %copy-done.15, ...), custom_call_target="tpu_custom_call" | custom-call | flops 2415919104 | bytes 4194304 | tf_op jit(solution)/shard_map/pallas_call | solution.py:214
  74.5 0.0 collective-permute-done.4.refs_4_.refs_2_
  74.5 1.9 %collective-permute-start.6 = (bf16[2,256,256]{2,1,0:T(8,128)(2,1)S(1)}, bf16[2,256,256]{2,1,0:T(8,128)(2,1)S(1)}, u32[]{:S(2)}, u32[]{:S(2)}) collective-permute-start(bf16[2,256,256]{2,1,0:T(8,128)(2,1)S(1)} %slice.17), channel_id=1, source_target_pairs={{0,4},{4,8},{8,12},{12,16},{16,20},{20,24},{24,28},{28,0},{32,36},... | collective-permute-start | bytes 786440 | tf_op jit(solution)/shard_map/ppermute | solution.py:32
  76.5 0.0 copy-done.2
  76.5 2.9 %shard_map.58 = (f32[3,8,128,256]{3,2,1,0:T(8,128)S(1)}, f32[3,8,128,128]{3,2,1,0:T(8,128)S(1)}) custom-call(s32[200]{0:T(256)S(1)} %copy-done.12, bf16[4,128,1024]{2,1,0:T(8,128)(2,1)S(1)} %all-to-all-done.refs_1_, bf16[4,256,256]{2,1,0:T(8,128)(2,1)S(1)} %collective-permute-done.2.refs_2_, bf16[4,256,256]{2,1,0:T(8,128)(2,1)S(1)} %collective-permute-done.3.refs_3_, ...), custom_call_target="tpu_custom_call" | custom-call | flops 1610612736 | bytes 4194304 | tf_op jit(solution)/shard_map/pallas_call | solution.py:214
  79.3 0.0 collective-permute-done.5.refs_5_.refs_3_
  79.4 5.5 %collective-permute-start.7 = (bf16[2,256,256]{2,1,0:T(8,128)(2,1)S(1)}, bf16[2,256,256]{2,1,0:T(8,128)(2,1)S(1)}, u32[]{:S(2)}, u32[]{:S(2)}) collective-permute-start(bf16[2,256,256]{2,1,0:T(8,128)(2,1)S(1)} %slice.18), channel_id=1, source_target_pairs={{0,28},{4,0},{8,4},{12,8},{16,12},{20,16},{24,20},{28,24},{32,60},... | collective-permute-start | bytes 786440 | tf_op jit(solution)/shard_map/ppermute | solution.py:32
  84.9 2.9 %shard_map.59 = (f32[3,8,128,256]{3,2,1,0:T(8,128)S(1)}, f32[3,8,128,128]{3,2,1,0:T(8,128)S(1)}) custom-call(s32[200]{0:T(256)S(1)} %copy-done.12, bf16[4,128,1024]{2,1,0:T(8,128)(2,1)S(1)} %all-to-all-done.refs_1_, bf16[4,256,256]{2,1,0:T(8,128)(2,1)S(1)} %collective-permute-done.4.refs_4_.refs_2_, ...), custom_call_target="tpu_custom_call" | custom-call | flops 1610612736 | bytes 4194304 | tf_op jit(solution)/shard_map/pallas_call | solution.py:214
  87.8 0.0 collective-permute-done.6
  87.8 0.4 collective-permute-done.7
  88.2 5.1 %shard_map.60 = bf16[4,128,1152]{2,1,0:T(8,128)(2,1)} custom-call(s32[200]{0:T(256)S(1)} %copy-done.12, bf16[4,128,1024]{2,1,0:T(8,128)(2,1)S(1)} %all-to-all-done.refs_1_, bf16[4,256,256]{2,1,0:T(8,128)(2,1)S(1)} %constant_dynamic-update-slice_fusion.refs_6_.refs_2_, f32[3,8,128,256]{3,2,1,0:T(8,128)S(1)} %get-tuple-element.17.refs_3_, ...), custom_call_target="tpu_custom_call" | custom-call | flops 805306368 | bytes 4194304 | tf_op jit(solution)/shard_map/pallas_call | solution.py:214
  93.4 0.0 copy-start.11
  93.4 7.8 %all-to-all-start.1 = ((bf16[4,128,1152]{2,1,0:T(8,128)(2,1)}), bf16[4,128,1152]{2,1,0:T(8,128)(2,1)S(1)}, u32[]{:S(2)}, u32[]{:S(2)}) async-start(bf16[4,128,1152]{2,1,0:T(8,128)(2,1)} %shard_map.60), calls=%async_computation.1 | async-start | bytes 2359296 | tf_op jit(solution)/shard_map/all_to_all | solution.py:40
  101.2 0.0 copy-done.11
  101.2 0.0 copy-done.13
  101.2 0.0 copy-start.6
  101.2 1.1 copy-done.6
  102.3 1.0 copy-done.16
  103.3 3.7 %shard_map.55.own1_ref = bf16[1,128,1152]{2,1,0:T(8,128)(2,1)S(1)} custom-call(s32[200]{0:T(256)S(1)} %copy-done.13, bf16[1,128,1024]{2,1,0:T(8,128)(2,1)S(1)} %bitcast.12, bf16[4,256,256]{2,1,0:T(8,128)(2,1)S(1)} %copy-done.6, bf16[4,256,256]{2,1,0:T(8,128)(2,1)S(1)} %copy-done.16, bf16[4,256,256]{2,1,0:T(8,128)(2,1)} %collective-permute-done.1.refs_4_), custom_call_target="tpu_custom_call" | custom-call | flops 805306368 | bytes 4194304 | tf_op jit(solution)/shard_map/pallas_call | solution.py:214
  107.0 0.0 copy-start.7
  107.0 0.7 copy-done.7
  107.7 0.0 copy-done.3
  107.7 3.7 %shard_map.56.own2_ref = bf16[1,128,1152]{2,1,0:T(8,128)(2,1)S(1)} custom-call(s32[200]{0:T(256)S(1)} %copy-done.13, bf16[1,128,1024]{2,1,0:T(8,128)(2,1)S(1)} %bitcast.13, bf16[4,256,256]{2,1,0:T(8,128)(2,1)S(1)} %collective-permute-done.2.refs_2_, bf16[4,256,256]{2,1,0:T(8,128)(2,1)S(1)} %copy-done.3, ...), custom_call_target="tpu_custom_call" | custom-call | flops 1342177280 | bytes 4194304 | tf_op jit(solution)/shard_map/pallas_call | solution.py:214
  111.4 0.0 copy-start.9
  111.4 0.7 copy-done.9
  112.1 0.0 all-to-all-done.1.part_ref
  112.2 2.2 %copy-done = bf16[1024,2048]{1,0:T(8,128)(2,1)S(1)} copy-done((bf16[1024,2048]{1,0:T(8,128)(2,1)S(1)}, bf16[1024,2048]{1,0:T(8,128)(2,1)}, u32[]{:S(2)}) %copy-start) | copy-done | bytes 4194328
  114.3 1.0 copy-done.8
  115.3 1.0 copy-done.10
  116.3 2.0 %shard_map.61 = (bf16[128,1024]{1,0:T(8,128)(2,1)S(1)}, bf16[2,128,512]{2,1,0:T(8,128)(2,1)S(1)}) custom-call(s32[1]{0:T(128)} %bitcast.at_ref, s32[200]{0:T(256)S(1)} %copy-done.13, bf16[1,128,1152]{2,1,0:T(8,128)(2,1)S(1)} %copy-done.8, bf16[1,128,1152]{2,1,0:T(8,128)(2,1)S(1)} %copy-done.10, bf16[4,128,1152]{2,1,0:T(8,128)(2,1)S(1)} %all-to-all-done.1.part_ref, ...), custom_call_target="tpu_custom_call" | custom-call | flops 268435456 | bytes 5242880 | tf_op jit(solution)/shard_map/pallas_call | solution.py:263
  118.3 8.3 %collective-permute-start.8 = (bf16[2,128,512]{2,1,0:T(8,128)(2,1)S(1)}, bf16[2,128,512]{2,1,0:T(8,128)(2,1)S(1)}, u32[]{:S(2)}, u32[]{:S(2)}) collective-permute-start(bf16[2,128,512]{2,1,0:T(8,128)(2,1)S(1)} %get-tuple-element.20), channel_id=1, source_target_pairs={{0,1},{1,0},{2,3},{3,2},{4,5},{5,4},{6,7},{7,6},{8,9},{9,8},{10,11... | collective-permute-start | bytes 786440 | tf_op jit(solution)/shard_map/ppermute | solution.py:301
  126.6 0.0 copy-done.1
  126.6 0.5 shard_map.62
  127.1 0.7 collective-permute-done.8
  127.8 0.1 convert_add_fusion
  127.9 6.0 %collective-permute-start.9 = (bf16[128,512]{1,0:T(8,128)(2,1)S(1)}, bf16[128,512]{1,0:T(8,128)(2,1)S(1)}, u32[]{:S(2)}, u32[]{:S(2)}) collective-permute-start(bf16[128,512]{1,0:T(8,128)(2,1)S(1)} %fusion.2), channel_id=1, source_target_pairs={{0,2},{1,3},{2,0},{3,1},{4,6},{5,7},{6,4},{7,5},{8,10},{9,11},{10,... | collective-permute-start | bytes 393224 | tf_op jit(solution)/shard_map/ppermute | solution.py:306
  133.9 3.5 %collective-permute-done.9 = bf16[128,512]{1,0:T(8,128)(2,1)S(1)} collective-permute-done((bf16[128,512]{1,0:T(8,128)(2,1)S(1)}, bf16[128,512]{1,0:T(8,128)(2,1)S(1)}, u32[]{:S(2)}, u32[]{:S(2)}) %collective-permute-start.9) | collective-permute-done | bytes 131104 | tf_op jit(solution)/shard_map/ppermute | solution.py:306
  137.4 0.7 fusion.1
  (12 shorter events, 0.1 us)
Async XLA Ops:
  21.5 19.5 %copy-start.4 = (bf16[4,256,256]{2,1,0:T(8,128)(2,1)}, bf16[4,256,256]{2,1,0:T(8,128)(2,1)S(1)}, u32[]{:S(2)}) copy-start(bf16[4,256,256]{2,1,0:T(8,128)(2,1)S(1)} %all_gather.3.refs_2_) | copy-start | bytes 1572868
  21.5 15.5 %collective-permute-start = (bf16[4,256,256]{2,1,0:T(8,128)(2,1)S(1)}, bf16[4,256,256]{2,1,0:T(8,128)(2,1)S(1)}, u32[]{:S(2)}, u32[]{:S(2)}) collective-permute-start(bf16[4,256,256]{2,1,0:T(8,128)(2,1)S(1)} %all_gather.3.refs_2_), channel_id=1, source_target_pairs={{0,4},{4,8},{8,12},{12,16},{16,20},{20,24},{24,28},{28,0},{32,36},... | collective-permute-start | bytes 1572872 | tf_op jit(solution)/shard_map/ppermute | solution.py:32
  24.7 20.3 %collective-permute-start.1 = (bf16[4,256,256]{2,1,0:T(8,128)(2,1)S(1)}, bf16[4,256,256]{2,1,0:T(8,128)(2,1)}, u32[]{:S(2)}, u32[]{:S(2)}) collective-permute-start(bf16[4,256,256]{2,1,0:T(8,128)(2,1)S(1)} %all_gather.3.refs_2_), channel_id=1, source_target_pairs={{0,28},{4,0},{8,4},{12,8},{16,12},{20,16},{24,20},{28,24},{32,60},... | collective-permute-start | bytes 1572872 | tf_op jit(solution)/shard_map/ppermute | solution.py:32
  37.0 4.0 %copy-start.14 = (bf16[4,256,256]{2,1,0:T(8,128)(2,1)}, bf16[4,256,256]{2,1,0:T(8,128)(2,1)S(1)}, u32[]{:S(2)}) copy-start(bf16[4,256,256]{2,1,0:T(8,128)(2,1)S(1)} %collective-permute-done.refs_3_) | copy-start | bytes 1572868
  37.0 14.1 %collective-permute-start.2 = (bf16[4,256,256]{2,1,0:T(8,128)(2,1)S(1)}, bf16[4,256,256]{2,1,0:T(8,128)(2,1)S(1)}, u32[]{:S(2)}, u32[]{:S(2)}) collective-permute-start(bf16[4,256,256]{2,1,0:T(8,128)(2,1)S(1)} %collective-permute-done.refs_3_), channel_id=1, source_target_pairs={{0,4},{4,8},{8,12},{12,16},{16,20},{20,24},{24,28},{28,0},{32,36},... | collective-permute-start | bytes 1572872 | tf_op jit(solution)/shard_map/ppermute | solution.py:32
  41.0 25.4 %all-to-all-start = ((bf16[4,128,1024]{2,1,0:T(8,128)(2,1)}), bf16[4,128,1024]{2,1,0:T(8,128)(2,1)S(1)}, u32[]{:S(2)}, u32[]{:S(2)}) async-start(bf16[4,128,1024]{2,1,0:T(8,128)(2,1)} %broadcast_in_dim.5), calls=%async_computation | async-start | bytes 2097152 | tf_op jit(solution)/shard_map/all_to_all | solution.py:40
  45.0 13.1 %collective-permute-start.3 = (bf16[4,256,256]{2,1,0:T(8,128)(2,1)}, bf16[4,256,256]{2,1,0:T(8,128)(2,1)S(1)}, u32[]{:S(2)}, u32[]{:S(2)}) collective-permute-start(bf16[4,256,256]{2,1,0:T(8,128)(2,1)} %collective-permute-done.1.refs_4_), channel_id=1, source_target_pairs={{0,28},{4,0},{8,4},{12,8},{16,12},{20,16},{24,20},{28,24},{32,60},... | collective-permute-start | bytes 1572872 | tf_op jit(solution)/shard_map/ppermute | solution.py:32
  51.1 23.4 %collective-permute-start.4 = (bf16[4,256,256]{2,1,0:T(8,128)(2,1)S(1)}, bf16[4,256,256]{2,1,0:T(8,128)(2,1)S(1)}, u32[]{:S(2)}, u32[]{:S(2)}) collective-permute-start(bf16[4,256,256]{2,1,0:T(8,128)(2,1)S(1)} %collective-permute-done.2.refs_2_), channel_id=1, source_target_pairs={{0,4},{4,8},{8,12},{12,16},{16,20},{20,24},{24,28},{28,0},{32,36},... | collective-permute-start | bytes 1572872 | tf_op jit(solution)/shard_map/ppermute | solution.py:32
  58.2 18.3 %copy-start.2 = (bf16[4,256,256]{2,1,0:T(8,128)(2,1)}, bf16[4,256,256]{2,1,0:T(8,128)(2,1)S(1)}, u32[]{:S(2)}) copy-start(bf16[4,256,256]{2,1,0:T(8,128)(2,1)S(1)} %collective-permute-done.3.refs_3_) | copy-start | bytes 1572868
  58.2 21.2 %collective-permute-start.5 = (bf16[4,256,256]{2,1,0:T(8,128)(2,1)S(1)}, bf16[4,256,256]{2,1,0:T(8,128)(2,1)S(1)}, u32[]{:S(2)}, u32[]{:S(2)}) collective-permute-start(bf16[4,256,256]{2,1,0:T(8,128)(2,1)S(1)} %collective-permute-done.3.refs_3_), channel_id=1, source_target_pairs={{0,28},{4,0},{8,4},{12,8},{16,12},{20,16},{24,20},{28,24},{32,60},... | collective-permute-start | bytes 1572872 | tf_op jit(solution)/shard_map/ppermute | solution.py:32
  66.5 1.0 copy-start.5
  67.5 0.7 copy-start.12
  68.2 1.0 copy-start.15
  74.5 13.2 %collective-permute-start.6 = (bf16[2,256,256]{2,1,0:T(8,128)(2,1)S(1)}, bf16[2,256,256]{2,1,0:T(8,128)(2,1)S(1)}, u32[]{:S(2)}, u32[]{:S(2)}) collective-permute-start(bf16[2,256,256]{2,1,0:T(8,128)(2,1)S(1)} %slice.17), channel_id=1, source_target_pairs={{0,4},{4,8},{8,12},{12,16},{16,20},{20,24},{24,28},{28,0},{32,36},... | collective-permute-start | bytes 786440 | tf_op jit(solution)/shard_map/ppermute | solution.py:32
  79.4 8.8 %collective-permute-start.7 = (bf16[2,256,256]{2,1,0:T(8,128)(2,1)S(1)}, bf16[2,256,256]{2,1,0:T(8,128)(2,1)S(1)}, u32[]{:S(2)}, u32[]{:S(2)}) collective-permute-start(bf16[2,256,256]{2,1,0:T(8,128)(2,1)S(1)} %slice.18), channel_id=1, source_target_pairs={{0,28},{4,0},{8,4},{12,8},{16,12},{20,16},{24,20},{28,24},{32,60},... | collective-permute-start | bytes 786440 | tf_op jit(solution)/shard_map/ppermute | solution.py:32
  93.4 7.8 %copy-start.11 = (bf16[128,1024]{1,0:T(8,128)(2,1)S(1)}, bf16[128,1024]{1,0:T(8,128)(2,1)}, u32[]{:S(2)}) copy-start(bf16[128,1024]{1,0:T(8,128)(2,1)} %param.5) | copy-start | bytes 786436
  93.4 7.8 %copy-start.13 = (s32[200]{0:T(256)S(1)}, s32[200]{0:T(256)}, u32[]{:S(2)}) copy-start(s32[200]{0:T(256)} %lists.1.refs_0_.list_ref) | copy-start | bytes 2404
  93.4 18.8 %all-to-all-start.1 = ((bf16[4,128,1152]{2,1,0:T(8,128)(2,1)}), bf16[4,128,1152]{2,1,0:T(8,128)(2,1)S(1)}, u32[]{:S(2)}, u32[]{:S(2)}) async-start(bf16[4,128,1152]{2,1,0:T(8,128)(2,1)} %shard_map.60), calls=%async_computation.1 | async-start | bytes 2359296 | tf_op jit(solution)/shard_map/all_to_all | solution.py:40
  101.2 6.5 %copy-start.3 = (bf16[4,256,256]{2,1,0:T(8,128)(2,1)S(1)}, bf16[4,256,256]{2,1,0:T(8,128)(2,1)}, u32[]{:S(2)}) copy-start(bf16[4,256,256]{2,1,0:T(8,128)(2,1)} %copy-done.2) | copy-start | bytes 1572868
  101.2 1.1 copy-start.6
  102.3 1.0 copy-start.16
  107.0 0.7 copy-start.7
  111.4 0.7 copy-start.9
  112.2 2.2 %copy-start = (bf16[1024,2048]{1,0:T(8,128)(2,1)S(1)}, bf16[1024,2048]{1,0:T(8,128)(2,1)}, u32[]{:S(2)}) copy-start(bf16[1024,2048]{1,0:T(8,128)(2,1)} %w_ref.3) | copy-start | bytes 12582916
  114.3 1.0 copy-start.8
  115.3 1.0 copy-start.10
  116.3 10.4 %copy-start.1 = (bf16[1024,2048]{1,0:T(8,128)(2,1)S(1)}, bf16[1024,2048]{1,0:T(8,128)(2,1)}, u32[]{:S(2)}) copy-start(bf16[1024,2048]{1,0:T(8,128)(2,1)} %w_ref.3) | copy-start | bytes 12582916
  118.3 9.5 %collective-permute-start.8 = (bf16[2,128,512]{2,1,0:T(8,128)(2,1)S(1)}, bf16[2,128,512]{2,1,0:T(8,128)(2,1)S(1)}, u32[]{:S(2)}, u32[]{:S(2)}) collective-permute-start(bf16[2,128,512]{2,1,0:T(8,128)(2,1)S(1)} %get-tuple-element.20), channel_id=1, source_target_pairs={{0,1},{1,0},{2,3},{3,2},{4,5},{5,4},{6,7},{7,6},{8,9},{9,8},{10,11... | collective-permute-start | bytes 786440 | tf_op jit(solution)/shard_map/ppermute | solution.py:301
  127.9 9.5 %collective-permute-start.9 = (bf16[128,512]{1,0:T(8,128)(2,1)S(1)}, bf16[128,512]{1,0:T(8,128)(2,1)S(1)}, u32[]{:S(2)}, u32[]{:S(2)}) collective-permute-start(bf16[128,512]{1,0:T(8,128)(2,1)S(1)} %fusion.2), channel_id=1, source_target_pairs={{0,2},{1,3},{2,0},{3,1},{4,6},{5,7},{6,4},{7,5},{8,10},{9,11},{10,... | collective-permute-start | bytes 393224 | tf_op jit(solution)/shard_map/ppermute | solution.py:306
